TPU v7x, 32 devices: a whole 2x2x4 slice. The times are simulated.
32 devices in a mesh: groups: 2 (over y), ctx: 4 (over z), head: 2 (over x), rep: 2 (over core).
Axes of the slice: x: 2, y: 2, z: 4, core: 2. Of those that a mesh axis runs over, the one named last changes fastest.
Arguments:
- queries: bfloat16 [2048, 4096], P(('groups', 'ctx'), ('head', 'rep')), parts along dimension 0, may hold values from -24 to 24
- keys: bfloat16 [2048, 1024], P(('groups', 'ctx'), ('head', 'rep')), parts along dimension 0, may hold values from -6 to 6
- values: bfloat16 [2048, 1024], P(('groups', 'ctx'), ('head', 'rep')), parts along dimension 0, may hold values from -6 to 6
- span_order: int32 [8], replicated, may hold values from 0 to 7, as said below
Outputs:
- attended: bfloat16 [2048, 4096], P(('groups', 'ctx'), ('head', 'rep')), parts along dimension 0
There are 2 independent parts, one for each index of `groups`. A program takes and returns all parts, laid end to end along the dimension named above; an argument that names none is the same for every part. Nothing has to cross between parts.
Inputs may be any that keep to these rules, and one draw needn't show every extreme that they name: `span_order`: A permutation of the spans in which entries 2 d and 2 d + 1 are c and 7 - c for some c.
All inputs are finite; a program needn't handle non-finite values.
Results may differ from a plain program's by a relative error of at most 0.0047.
Values may be sent and summed in bfloat16 or wider, within the bound.
A program may use at most 64 MiB of HBM per device.

v0:
```python
import functools
import math

import jax
import jax.numpy as jnp
from jax import lax
from jax.experimental import pallas as pl
from jax.experimental.pallas import tpu as pltpu
from jax.sharding import PartitionSpec as P

HEAD_SIZE = 128
MASKED = -1e30
MESH = pl.DeviceIdType.MESH
KEY, VALUE = 0, 1


def attend(
    n, order_hbm, q_hbm, k_hbm, v_hbm, out_ref,
    order_ref, q_ref, k_ref, v_ref, stack_ref, p_ref, top_ref, acc_ref,
    load_sem, send_sem, recv_sem,
):
    me = lax.axis_index("ctx")
    rows, q_cols = q_ref.shape
    span = rows // 2
    kv_heads = k_ref.shape[2] // HEAD_SIZE
    group = q_cols // HEAD_SIZE // kv_heads
    exponent_scale = math.log2(math.e) / math.sqrt(HEAD_SIZE)
    buffers = (k_ref, v_ref)

    load_k = pltpu.make_async_copy(k_hbm, k_ref.at[me], load_sem.at[0])
    load_v = pltpu.make_async_copy(v_hbm, v_ref.at[me], load_sem.at[1])
    load_order = pltpu.make_async_copy(order_hbm, order_ref, load_sem.at[3])
    load_q = pltpu.make_async_copy(q_hbm, q_ref, load_sem.at[2])
    load_k.start()
    load_v.start()
    load_q.start()
    load_order.start()

    major = jnp.where(me < n // 2, -1, 1)

    def inside(index):
        return (index >= 0) & (index < n)

    barrier = pltpu.get_barrier_semaphore()
    for way in (-1, 1):
        @pl.when(inside(me + way))
        def _():
            pl.semaphore_signal(barrier, inc=1, device_id={"ctx": me + way}, device_id_type=MESH)

    pl.semaphore_wait(barrier, jnp.where(me > 0, 1, 0) + jnp.where(me < n - 1, 1, 0))

    def hop(way, kind, step, block):
        lane = (way + 1) // 2
        return pltpu.make_async_remote_copy(
            src_ref=buffers[kind].at[block],
            dst_ref=buffers[kind].at[block],
            send_sem=send_sem.at[lane, kind, step],
            recv_sem=recv_sem.at[lane, kind, step],
            device_id={"ctx": jnp.clip(me + way, 0, n - 1)},
            device_id_type=MESH,
        )

    def arrive(kind, step):
        for way in (major, -major):
            @pl.when(inside(me - way * step))
            def _():
                hop(way, kind, step - 1, me - way * step).wait_recv()

                @pl.when(inside(me + way))
                def _():
                    hop(way, kind, step, me - way * step).start()

    for kind, load in ((KEY, load_k), (VALUE, load_v)):
        load.wait()
        for way in (major, -major):
            @pl.when(inside(me + way))
            def _():
                hop(way, kind, 0, me).start()

    load_q.wait()
    load_order.wait()

    def columns(head):
        return pl.ds(head * HEAD_SIZE, HEAD_SIZE)

    def low_first(block):
        return order_ref[2 * block] < order_ref[2 * block + 1]

    def low_span(block):
        return jnp.minimum(order_ref[2 * block], order_ref[2 * block + 1])

    def low_high(ref, block, head):
        first, second = ref[block, :span, columns(head)], ref[block, span:, columns(head)]
        swap = low_first(block)
        return jnp.where(swap, first, second), jnp.where(swap, second, first)

    def score(head, part, keys):
        queries = stack_ref[head, part] if isinstance(part, int) else part
        return lax.dot_general(
            queries, keys, (((1,), (1,)), ((), ())), preferred_element_type=jnp.float32
        )

    def peak(scores):
        return jnp.max(scores, axis=1, keepdims=True)

    def weights_of(scores, top):
        return jnp.exp2((scores - top) * exponent_scale).astype(jnp.bfloat16)

    def keep(ref, value):
        ref[...] = jnp.broadcast_to(value, (group * span, HEAD_SIZE))

    def with_ones(values):
        return jnp.concatenate([values, jnp.ones_like(values)], axis=1)

    def product(weights, values):
        return jnp.dot(weights, with_ones(values), preferred_element_type=jnp.float32)

    mine_first = low_first(me)
    for head in range(kv_heads):
        for member in range(group):
            column = columns(head * group + member)
            first, second = q_ref[:span, column], q_ref[span:, column]
            stack_ref[head, 0, member * span : (member + 1) * span] = jnp.where(mine_first, first, second)
            stack_ref[head, 1, member * span : (member + 1) * span] = jnp.where(mine_first, second, first)

    tall = (group * span, span)
    row = lax.rem(lax.broadcasted_iota(jnp.int32, tall, 0), span)
    bias = jnp.where(lax.broadcasted_iota(jnp.int32, tall, 1) <= row, 0.0, MASKED)
    for head in range(kv_heads):
        key_low, key_high = low_high(k_ref, me, head)
        value_low, value_high = low_high(v_ref, me, head)
        low = score(head, 0, key_low) + bias
        low_top = peak(low)
        keep(top_ref.at[head, 0], low_top)
        acc_ref[head, 0] = product(weights_of(low, low_top), value_low)
        cross = score(head, 1, key_low)
        high = score(head, 1, key_high) + bias
        high_top = jnp.maximum(peak(cross), peak(high))
        keep(top_ref.at[head, 1], high_top)
        acc_ref[head, 1] = product(weights_of(cross, high_top), value_low) + product(
            weights_of(high, high_top), value_high
        )

    def weigh(block):
        earlier = low_span(block) < low_span(me)
        for head in range(kv_heads):
            key_low, key_high = low_high(k_ref, block, head)
            cross = score(head, 1, key_low)
            other = score(
                head,
                jnp.where(earlier, stack_ref[head, 0], stack_ref[head, 1]),
                jnp.where(earlier, key_low, key_high),
            )
            other_top = peak(other)
            old_low, old_high = top_ref[head, 0][:, :1], top_ref[head, 1][:, :1]
            low_top = jnp.maximum(old_low, jnp.where(earlier, other_top, MASKED))
            high_top = jnp.maximum(
                jnp.maximum(old_high, peak(cross)), jnp.where(earlier, MASKED, other_top)
            )
            keep(top_ref.at[head, 0], low_top)
            keep(top_ref.at[head, 1], high_top)
            acc_ref[head, 0] *= jnp.exp2((old_low - low_top) * exponent_scale)
            acc_ref[head, 1] *= jnp.exp2((old_high - high_top) * exponent_scale)
            p_ref[head, 0] = weights_of(cross, high_top)
            p_ref[head, 1] = weights_of(other, jnp.where(earlier, low_top, high_top))

    def gather(block):
        earlier = low_span(block) < low_span(me)
        for head in range(kv_heads):
            value_low, value_high = low_high(v_ref, block, head)
            cross = product(p_ref[head, 0], value_low)
            other = product(p_ref[head, 1], jnp.where(earlier, value_low, value_high))
            acc_ref[head, 0] += jnp.where(earlier, other, 0.0)
            acc_ref[head, 1] += cross + jnp.where(earlier, 0.0, other)

    def turn(step, carry):
        arrive(KEY, step)

        @pl.when(inside(me - major * step))
        def _():
            weigh(me - major * step)

        arrive(VALUE, step)

        @pl.when(inside(me - major * step))
        def _():
            gather(me - major * step)

        @pl.when(inside(me + major * step))
        def _():
            weigh(me + major * step)
            gather(me + major * step)

        return carry

    lax.fori_loop(1, n, turn, 0)

    for head in range(kv_heads):
        for member in range(group):
            column = columns(head * group + member)
            part = pl.ds(member * span, span)
            low = acc_ref[head, 0, part, :HEAD_SIZE] / acc_ref[head, 0, part, HEAD_SIZE:]
            high = acc_ref[head, 1, part, :HEAD_SIZE] / acc_ref[head, 1, part, HEAD_SIZE:]
            out_ref[:span, column] = jnp.where(mine_first, low, high).astype(out_ref.dtype)
            out_ref[span:, column] = jnp.where(mine_first, high, low).astype(out_ref.dtype)

    def drain(step, carry):
        for kind in (KEY, VALUE):
            for way in (major, -major):
                @pl.when(inside(me - way * step) & inside(me + way))
                def _():
                    hop(way, kind, step, me - way * step).wait_send()
        return carry

    lax.fori_loop(0, n - 1, drain, 0)


def shards(n, queries, keys, values, span_order):
    rows, q_cols = queries.shape
    span = rows // 2
    kv_heads = keys.shape[1] // HEAD_SIZE
    tall = q_cols // HEAD_SIZE // kv_heads * span
    inputs = [pltpu.with_memory_space_constraint(x, pltpu.HBM) for x in (span_order, queries, keys, values)]
    return pl.pallas_call(
        functools.partial(attend, n),
        out_shape=jax.ShapeDtypeStruct((rows, q_cols), jnp.bfloat16),
        in_specs=[pl.BlockSpec(memory_space=pltpu.HBM)] * 4,
        out_specs=pl.BlockSpec(memory_space=pltpu.VMEM),
        scratch_shapes=[
            pltpu.SMEM(span_order.shape, jnp.int32),
            pltpu.VMEM((rows, q_cols), jnp.bfloat16),
            pltpu.VMEM((n,) + keys.shape, jnp.bfloat16),
            pltpu.VMEM((n,) + values.shape, jnp.bfloat16),
            pltpu.VMEM((kv_heads, 2, tall, HEAD_SIZE), jnp.bfloat16),
            pltpu.VMEM((kv_heads, 2, tall, span), jnp.bfloat16),
            pltpu.VMEM((kv_heads, 2, tall, HEAD_SIZE), jnp.float32),
            pltpu.VMEM((kv_heads, 2, tall, 2 * HEAD_SIZE), jnp.float32),
            pltpu.SemaphoreType.DMA((4,)),
            pltpu.SemaphoreType.DMA((2, 2, n)),
            pltpu.SemaphoreType.DMA((2, 2, n)),
        ],
        compiler_params=pltpu.CompilerParams(
            collective_id=0, has_side_effects=True, vmem_limit_bytes=32 * 2**20
        ),
    )(*inputs)


def solution(mesh):
    split = P(("groups", "ctx"), ("head", "rep"))
    return jax.shard_map(
        functools.partial(shards, mesh.shape["ctx"]),
        mesh=mesh,
        in_specs=(split, split, split, P()),
        out_specs=split,
        check_vma=False,
    )
```

profile of v0, /device:TPU:0, one launch (start us, length us, event | category | flops | bytes accessed | tf_op | source)
XLA Modules:
  0.0 23.7 jit_solution(14800667227633123744)
XLA Ops:
  0.0 22.9 %shard_map.46 = bf16[256,1024]{1,0:T(8,128)(2,1)S(1)} custom-call(s32[8]{0:T(128)} %order_hbm.1, bf16[256,1024]{1,0:T(8,128)(2,1)} %q_hbm.1, bf16[256,256]{1,0:T(8,128)(2,1)} %k_hbm.1, bf16[256,256]{1,0:T(8,128)(2,1)} %v_hbm.1), custom_call_target="tpu_custom_call" | custom-call | tf_op jit(solution)/shard_map/pallas_call | solution.py:224
  22.9 0.8 %copy.6 = bf16[256,1024]{1,0:T(8,128)(2,1)} copy(bf16[256,1024]{1,0:T(8,128)(2,1)S(1)} %shard_map.46) | data formatting | bytes 1048576
where the time goes:
time: 23.8 us; the launch traced here: 23.7 us
  Pallas kernels  22.9 us (96%)
  local copies, waits for them, and re-layouts  0.8 us (3%)
    pallas_call x1, Pallas kernels, shards(): pl.pallas_call(functools.partial(attend, n), out_shape=jax.ShapeDtypeStru...  22.9 us
    unnamed x1, local copies, waits for them, and re-layouts  0.8 us

commit v1 on v0

v1 whole, which is shorter than its diff:
```python
import functools
import math

import jax
import jax.numpy as jnp
from jax import lax
from jax.experimental import pallas as pl
from jax.experimental.pallas import tpu as pltpu
from jax.sharding import PartitionSpec as P

HEAD_SIZE = 128
MASKED = -1e30
MESH = pl.DeviceIdType.MESH
KEY, VALUE = 0, 1


def attend(
    n, order_hbm, q_hbm, k_hbm, v_hbm, out_ref,
    order_ref, q_ref, k_ref, v_ref, stack_ref, p_ref, top_ref, sum_ref, acc_ref,
    load_sem, send_sem, recv_sem,
):
    me = lax.axis_index("ctx")
    rows, q_cols = q_ref.shape
    span = rows // 2
    kv_heads = k_ref.shape[1]
    group = q_cols // HEAD_SIZE // kv_heads
    tall = group * span
    exponent_scale = math.log2(math.e) / math.sqrt(HEAD_SIZE)
    buffers = (k_ref, v_ref)
    chunks = [(kind, head) for head in range(kv_heads) for kind in (KEY, VALUE)]

    def columns(head):
        return pl.ds(head * HEAD_SIZE, HEAD_SIZE)

    loads = {
        (kind, head): pltpu.make_async_copy(
            (k_hbm, v_hbm)[kind].at[:, columns(head)], buffers[kind].at[me, head], load_sem.at[2 * head + kind]
        )
        for kind, head in chunks
    }
    load_order = pltpu.make_async_copy(order_hbm, order_ref, load_sem.at[2 * kv_heads])
    load_q = pltpu.make_async_copy(q_hbm, q_ref, load_sem.at[2 * kv_heads + 1])
    for chunk in chunks:
        loads[chunk].start()
    load_q.start()
    load_order.start()

    major = jnp.where(me < n // 2, -1, 1)

    def inside(index):
        return (index >= 0) & (index < n)

    barrier = pltpu.get_barrier_semaphore()
    for way in (-1, 1):
        @pl.when(inside(me + way))
        def _():
            pl.semaphore_signal(barrier, inc=1, device_id={"ctx": me + way}, device_id_type=MESH)

    pl.semaphore_wait(barrier, jnp.where(me > 0, 1, 0) + jnp.where(me < n - 1, 1, 0))

    def hop(way, kind, head, step, block):
        lane = (way + 1) // 2
        return pltpu.make_async_remote_copy(
            src_ref=buffers[kind].at[block, head],
            dst_ref=buffers[kind].at[block, head],
            send_sem=send_sem.at[lane, kind, head, step],
            recv_sem=recv_sem.at[lane, kind, head, step],
            device_id={"ctx": jnp.clip(me + way, 0, n - 1)},
            device_id_type=MESH,
        )

    def arrive(way, kind, head, step):
        hop(way, kind, head, step - 1, me - way * step).wait_recv()

        @pl.when(inside(me + way))
        def _():
            hop(way, kind, head, step, me - way * step).start()

    for kind, head in chunks:
        loads[kind, head].wait()
        for way in (major, -major):
            @pl.when(inside(me + way))
            def _():
                hop(way, kind, head, 0, me).start()

    load_q.wait()
    load_order.wait()

    def low_first(block):
        return order_ref[2 * block] < order_ref[2 * block + 1]

    def low_span(block):
        return jnp.minimum(order_ref[2 * block], order_ref[2 * block + 1])

    def low_high(ref, block, head):
        first, second = ref[block, head, :span], ref[block, head, span:]
        swap = low_first(block)
        return jnp.where(swap, first, second), jnp.where(swap, second, first)

    def score(queries, keys):
        return lax.dot_general(
            queries, keys, (((1,), (1,)), ((), ())), preferred_element_type=jnp.float32
        )

    def peak(scores):
        return jnp.broadcast_to(jnp.max(scores, axis=1, keepdims=True), (tall, HEAD_SIZE))

    def weights_of(scores, top):
        return jnp.exp2((scores - top) * exponent_scale).astype(jnp.bfloat16)

    mine_first = low_first(me)

    def stored(low, high):
        return jnp.where(mine_first, low, high), jnp.where(mine_first, high, low)

    def mixer(earlier, low, high):
        none = jnp.zeros_like(low)
        to_low = jnp.concatenate([none, jnp.where(earlier, low, none)], axis=0)
        to_high = jnp.concatenate([low, jnp.where(earlier, none, high)], axis=0)
        return jnp.concatenate(stored(to_low, to_high), axis=1)

    def product(weights, values):
        return jnp.dot(weights, values, preferred_element_type=jnp.float32)

    for head in range(kv_heads):
        for member in range(group):
            column = columns(head * group + member)
            low, high = stored(q_ref[:span, column], q_ref[span:, column])
            stack_ref[head, 0, member * span : (member + 1) * span] = low
            stack_ref[head, 1, member * span : (member + 1) * span] = high

    row = lax.rem(lax.broadcasted_iota(jnp.int32, (tall, span), 0), span)
    bias = jnp.where(lax.broadcasted_iota(jnp.int32, (tall, span), 1) <= row, 0.0, MASKED)
    ones = jnp.ones((span, HEAD_SIZE), jnp.bfloat16)
    for head in range(kv_heads):
        key_low, key_high = low_high(k_ref, me, head)
        value_low, value_high = low_high(v_ref, me, head)
        low = score(stack_ref[head, 0], key_low) + bias
        low_top = peak(low)
        top_ref[head, 0] = low_top
        low = weights_of(low, low_top)
        cross = score(stack_ref[head, 1], key_low)
        high = score(stack_ref[head, 1], key_high) + bias
        high_top = jnp.maximum(peak(cross), peak(high))
        top_ref[head, 1] = high_top
        high = jnp.concatenate([weights_of(cross, high_top), weights_of(high, high_top)], axis=1)
        low = product(low, jnp.concatenate([value_low, ones], axis=1))
        high = product(high, jnp.concatenate(
            [jnp.concatenate([value_low, value_high], axis=0), jnp.concatenate([ones, ones], axis=0)], axis=1
        ))
        acc_ref[head] = jnp.concatenate(stored(low[:, :HEAD_SIZE], high[:, :HEAD_SIZE]), axis=1)
        sum_ref[head] = jnp.concatenate(stored(low[:, HEAD_SIZE:], high[:, HEAD_SIZE:]), axis=1)

    def weigh(block, head):
        earlier = low_span(block) < low_span(me)
        key_low, key_high = low_high(k_ref, block, head)
        cross = score(stack_ref[head, 1], key_low)
        other = score(
            jnp.where(earlier, stack_ref[head, 0], stack_ref[head, 1]),
            jnp.where(earlier, key_low, key_high),
        )
        other_top = peak(other)
        old_low, old_high = top_ref[head, 0], top_ref[head, 1]
        low_top = jnp.maximum(old_low, jnp.where(earlier, other_top, MASKED))
        high_top = jnp.maximum(
            jnp.maximum(old_high, peak(cross)), jnp.where(earlier, MASKED, other_top)
        )
        top_ref[head, 0] = low_top
        top_ref[head, 1] = high_top
        weights = jnp.concatenate(
            [weights_of(cross, high_top), weights_of(other, jnp.where(earlier, low_top, high_top))], axis=1
        )
        p_ref[head] = weights
        fade = jnp.concatenate(
            stored(
                jnp.exp2((old_low - low_top) * exponent_scale),
                jnp.exp2((old_high - high_top) * exponent_scale),
            ),
            axis=1,
        )
        acc_ref[head] *= fade
        sum_ref[head] = sum_ref[head] * fade + product(weights, mixer(earlier, ones, ones))

    def gathered(block, head):
        earlier = low_span(block) < low_span(me)
        return acc_ref[head] + product(p_ref[head], mixer(earlier, *low_high(v_ref, block, head)))

    def turn(step, head):
        for way in (major, -major):
            @pl.when(inside(me - way * step))
            def _():
                arrive(way, KEY, head, step)
                weigh(me - way * step, head)
                arrive(way, VALUE, head, step)
                acc_ref[head] = gathered(me - way * step, head)

    def steps(step, carry):
        for head in range(kv_heads):
            turn(step, head)
        return carry

    lax.fori_loop(1, n - 1, steps, 0)

    def finish(head, total):
        result = (total * sum_ref[head]).astype(out_ref.dtype)
        for member in range(group):
            column = columns(head * group + member)
            part = slice(member * span, (member + 1) * span)
            out_ref[:span, column] = result[part, :HEAD_SIZE]
            out_ref[span:, column] = result[part, HEAD_SIZE:]

    last = me - major * (n - 1)
    for head in range(kv_heads):
        @pl.when(inside(last))
        def _():
            hop(major, KEY, head, n - 2, last).wait_recv()
            weigh(last, head)
            sum_ref[head] = 1.0 / sum_ref[head]
            hop(major, VALUE, head, n - 2, last).wait_recv()
            finish(head, gathered(last, head))

        @pl.when(jnp.logical_not(inside(last)))
        def _():
            sum_ref[head] = 1.0 / sum_ref[head]
            finish(head, acc_ref[head])

    def drain(step, carry):
        for kind, head in chunks:
            for way in (major, -major):
                @pl.when(inside(me - way * step) & inside(me + way))
                def _():
                    hop(way, kind, head, step, me - way * step).wait_send()
        return carry

    lax.fori_loop(0, n - 1, drain, 0)


def shards(n, queries, keys, values, span_order):
    rows, q_cols = queries.shape
    span = rows // 2
    kv_heads = keys.shape[1] // HEAD_SIZE
    tall = q_cols // HEAD_SIZE // kv_heads * span
    inputs = [pltpu.with_memory_space_constraint(x, pltpu.HBM) for x in (span_order, queries, keys, values)]
    return pl.pallas_call(
        functools.partial(attend, n),
        out_shape=jax.ShapeDtypeStruct((rows, q_cols), jnp.bfloat16),
        in_specs=[pl.BlockSpec(memory_space=pltpu.HBM)] * 4,
        out_specs=pl.BlockSpec(memory_space=pltpu.VMEM),
        scratch_shapes=[
            pltpu.SMEM(span_order.shape, jnp.int32),
            pltpu.VMEM((rows, q_cols), jnp.bfloat16),
            pltpu.VMEM((n, kv_heads, rows, HEAD_SIZE), jnp.bfloat16),
            pltpu.VMEM((n, kv_heads, rows, HEAD_SIZE), jnp.bfloat16),
            pltpu.VMEM((kv_heads, 2, tall, HEAD_SIZE), jnp.bfloat16),
            pltpu.VMEM((kv_heads, tall, 2 * span), jnp.bfloat16),
            pltpu.VMEM((kv_heads, 2, tall, HEAD_SIZE), jnp.float32),
            pltpu.VMEM((kv_heads, tall, 2 * HEAD_SIZE), jnp.float32),
            pltpu.VMEM((kv_heads, tall, 2 * HEAD_SIZE), jnp.float32),
            pltpu.SemaphoreType.DMA((2 * kv_heads + 2,)),
            pltpu.SemaphoreType.DMA((2, 2, kv_heads, n)),
            pltpu.SemaphoreType.DMA((2, 2, kv_heads, n)),
        ],
        compiler_params=pltpu.CompilerParams(
            collective_id=0, has_side_effects=True, vmem_limit_bytes=32 * 2**20
        ),
    )(*inputs)


def solution(mesh):
    split = P(("groups", "ctx"), ("head", "rep"))
    return jax.shard_map(
        functools.partial(shards, mesh.shape["ctx"]),
        mesh=mesh,
        in_specs=(split, split, split, P()),
        out_specs=split,
        check_vma=False,
    )
```

time: 23.8 us -> 23.8 us (level)
  no operation moved by 1% of the time
where the time goes in v1:
time: 23.8 us; the launch traced here: 23.7 us
  Pallas kernels  22.9 us (96%)
  local copies, waits for them, and re-layouts  0.8 us (3%)
    pallas_call x1, Pallas kernels, shards(): pl.pallas_call(functools.partial(attend, n), out_shape=jax.ShapeDtypeStru...  22.9 us
    unnamed x1, local copies, waits for them, and re-layouts  0.8 us

profile of v1, /device:TPU:0, one launch (start us, length us, event | category | flops | bytes accessed | tf_op | source)
XLA Modules:
  0.0 23.7 jit_solution(3029969394825737705)
XLA Ops:
  0.0 22.9 %shard_map.46 = bf16[256,1024]{1,0:T(8,128)(2,1)S(1)} custom-call(s32[8]{0:T(128)} %order_hbm.1, bf16[256,1024]{1,0:T(8,128)(2,1)} %q_hbm.1, bf16[256,256]{1,0:T(8,128)(2,1)} %k_hbm.1, bf16[256,256]{1,0:T(8,128)(2,1)} %v_hbm.1), custom_call_target="tpu_custom_call" | custom-call | tf_op jit(solution)/shard_map/pallas_call | solution.py:244
  22.9 0.8 %copy.6 = bf16[256,1024]{1,0:T(8,128)(2,1)} copy(bf16[256,1024]{1,0:T(8,128)(2,1)S(1)} %shard_map.46) | data formatting | bytes 1048576

commit v2 on v1

--- a/solution.py
+++ b/solution.py
@@ -12,36 +12,42 @@
 MASKED = -1e30
 MESH = pl.DeviceIdType.MESH
 KEY, VALUE = 0, 1
+OWN, RELAYED = 0, 1
 
 
 def attend(
     n, order_hbm, q_hbm, k_hbm, v_hbm, out_ref,
-    order_ref, q_ref, k_ref, v_ref, stack_ref, p_ref, top_ref, sum_ref, acc_ref,
-    load_sem, send_sem, recv_sem,
+    order_ref, q_ref, kv_ref, stack_ref, p_ref, top_ref, sum_ref, acc_ref,
+    chunk_sem, load_sem, send_sem, entered_sem,
 ):
     me = lax.axis_index("ctx")
     rows, q_cols = q_ref.shape
     span = rows // 2
-    kv_heads = k_ref.shape[1]
+    per_block = kv_ref.shape[0] // n
+    kv_heads = per_block // 2
     group = q_cols // HEAD_SIZE // kv_heads
     tall = group * span
     exponent_scale = math.log2(math.e) / math.sqrt(HEAD_SIZE)
-    buffers = (k_ref, v_ref)
     chunks = [(kind, head) for head in range(kv_heads) for kind in (KEY, VALUE)]
 
     def columns(head):
         return pl.ds(head * HEAD_SIZE, HEAD_SIZE)
 
-    loads = {
-        (kind, head): pltpu.make_async_copy(
-            (k_hbm, v_hbm)[kind].at[:, columns(head)], buffers[kind].at[me, head], load_sem.at[2 * head + kind]
+    def place(kind, head, block):
+        return block * per_block + 2 * head + kind
+
+    loads = [
+        pltpu.make_async_copy(
+            (k_hbm, v_hbm)[kind].at[:, columns(head)],
+            kv_ref.at[place(kind, head, me)],
+            chunk_sem.at[place(kind, head, me)],
         )
         for kind, head in chunks
-    }
-    load_order = pltpu.make_async_copy(order_hbm, order_ref, load_sem.at[2 * kv_heads])
-    load_q = pltpu.make_async_copy(q_hbm, q_ref, load_sem.at[2 * kv_heads + 1])
-    for chunk in chunks:
-        loads[chunk].start()
+    ]
+    load_order = pltpu.make_async_copy(order_hbm, order_ref, load_sem.at[0])
+    load_q = pltpu.make_async_copy(q_hbm, q_ref, load_sem.at[1])
+    for load in loads:
+        load.start()
     load_q.start()
     load_order.start()
 
@@ -51,37 +57,49 @@
         return (index >= 0) & (index < n)
 
     barrier = pltpu.get_barrier_semaphore()
-    for way in (-1, 1):
-        @pl.when(inside(me + way))
-        def _():
-            pl.semaphore_signal(barrier, inc=1, device_id={"ctx": me + way}, device_id_type=MESH)
-
-    pl.semaphore_wait(barrier, jnp.where(me > 0, 1, 0) + jnp.where(me < n - 1, 1, 0))
-
-    def hop(way, kind, head, step, block):
-        lane = (way + 1) // 2
+
+    @pl.when(me < n - 1)
+    def _():
+        pl.semaphore_signal(barrier, inc=1, device_id={"ctx": me + 1}, device_id_type=MESH)
+
+    @pl.when(me > 0)
+    def _():
+        pl.semaphore_wait(barrier, 1)
+        pl.semaphore_signal(entered_sem, inc=1, device_id={"ctx": me - 1}, device_id_type=MESH)
+
+    def send(way, at, pool, count=None):
+        part = kv_ref.at[at] if count is None else kv_ref.at[pl.ds(at, count)]
         return pltpu.make_async_remote_copy(
-            src_ref=buffers[kind].at[block, head],
-            dst_ref=buffers[kind].at[block, head],
-            send_sem=send_sem.at[lane, kind, head, step],
-            recv_sem=recv_sem.at[lane, kind, head, step],
+            src_ref=part,
+            dst_ref=part,
+            send_sem=send_sem.at[pool],
+            recv_sem=chunk_sem.at[at],
             device_id={"ctx": jnp.clip(me + way, 0, n - 1)},
             device_id_type=MESH,
         )
 
+    def take(way, kind, head, step):
+        send(-way, place(kind, head, me - way * step), RELAYED).wait_recv()
+
     def arrive(way, kind, head, step):
-        hop(way, kind, head, step - 1, me - way * step).wait_recv()
+        take(way, kind, head, step)
 
         @pl.when(inside(me + way))
         def _():
-            hop(way, kind, head, step, me - way * step).start()
-
-    for kind, head in chunks:
-        loads[kind, head].wait()
-        for way in (major, -major):
-            @pl.when(inside(me + way))
-            def _():
-                hop(way, kind, head, 0, me).start()
+            send(way, place(kind, head, me - way * step), RELAYED).start()
+
+    for load, (kind, head) in zip(loads, chunks):
+        load.wait()
+
+        @pl.when(me > 0)
+        def _():
+            send(-1, place(kind, head, me), OWN).start()
+
+    @pl.when(me < n - 1)
+    def _():
+        pl.semaphore_wait(entered_sem, 1)
+        for kind, head in chunks:
+            send(1, place(kind, head, me), OWN).start()
 
     load_q.wait()
     load_order.wait()
@@ -92,8 +110,9 @@
     def low_span(block):
         return jnp.minimum(order_ref[2 * block], order_ref[2 * block + 1])
 
-    def low_high(ref, block, head):
-        first, second = ref[block, head, :span], ref[block, head, span:]
+    def low_high(kind, block, head):
+        at = place(kind, head, block)
+        first, second = kv_ref[at, :span], kv_ref[at, span:]
         swap = low_first(block)
         return jnp.where(swap, first, second), jnp.where(swap, second, first)
 
@@ -133,8 +152,8 @@
     bias = jnp.where(lax.broadcasted_iota(jnp.int32, (tall, span), 1) <= row, 0.0, MASKED)
     ones = jnp.ones((span, HEAD_SIZE), jnp.bfloat16)
     for head in range(kv_heads):
-        key_low, key_high = low_high(k_ref, me, head)
-        value_low, value_high = low_high(v_ref, me, head)
+        key_low, key_high = low_high(KEY, me, head)
+        value_low, value_high = low_high(VALUE, me, head)
         low = score(stack_ref[head, 0], key_low) + bias
         low_top = peak(low)
         top_ref[head, 0] = low_top
@@ -153,7 +172,7 @@
 
     def weigh(block, head):
         earlier = low_span(block) < low_span(me)
-        key_low, key_high = low_high(k_ref, block, head)
+        key_low, key_high = low_high(KEY, block, head)
         cross = score(stack_ref[head, 1], key_low)
         other = score(
             jnp.where(earlier, stack_ref[head, 0], stack_ref[head, 1]),
@@ -183,7 +202,7 @@
 
     def gathered(block, head):
         earlier = low_span(block) < low_span(me)
-        return acc_ref[head] + product(p_ref[head], mixer(earlier, *low_high(v_ref, block, head)))
+        return acc_ref[head] + product(p_ref[head], mixer(earlier, *low_high(VALUE, block, head)))
 
     def turn(step, head):
         for way in (major, -major):
@@ -213,10 +232,10 @@
     for head in range(kv_heads):
         @pl.when(inside(last))
         def _():
-            hop(major, KEY, head, n - 2, last).wait_recv()
+            take(major, KEY, head, n - 1)
             weigh(last, head)
             sum_ref[head] = 1.0 / sum_ref[head]
-            hop(major, VALUE, head, n - 2, last).wait_recv()
+            take(major, VALUE, head, n - 1)
             finish(head, gathered(last, head))
 
         @pl.when(jnp.logical_not(inside(last)))
@@ -224,15 +243,14 @@
             sum_ref[head] = 1.0 / sum_ref[head]
             finish(head, acc_ref[head])
 
-    def drain(step, carry):
-        for kind, head in chunks:
-            for way in (major, -major):
-                @pl.when(inside(me - way * step) & inside(me + way))
-                def _():
-                    hop(way, kind, head, step, me - way * step).wait_send()
-        return carry
-
-    lax.fori_loop(0, n - 1, drain, 0)
+    @pl.when((me > 0) & (me < n - 1))
+    def _():
+        send(1, 0, OWN, 2 * per_block).wait_send()
+        send(1, 0, RELAYED, (n - 1) * per_block).wait_send()
+
+    @pl.when((me == 0) | (me == n - 1))
+    def _():
+        send(1, 0, OWN, per_block).wait_send()
 
 
 def shards(n, queries, keys, values, span_order):
@@ -249,16 +267,16 @@
         scratch_shapes=[
             pltpu.SMEM(span_order.shape, jnp.int32),
             pltpu.VMEM((rows, q_cols), jnp.bfloat16),
-            pltpu.VMEM((n, kv_heads, rows, HEAD_SIZE), jnp.bfloat16),
-            pltpu.VMEM((n, kv_heads, rows, HEAD_SIZE), jnp.bfloat16),
+            pltpu.VMEM((2 * kv_heads * n, rows, HEAD_SIZE), jnp.bfloat16),
             pltpu.VMEM((kv_heads, 2, tall, HEAD_SIZE), jnp.bfloat16),
             pltpu.VMEM((kv_heads, tall, 2 * span), jnp.bfloat16),
             pltpu.VMEM((kv_heads, 2, tall, HEAD_SIZE), jnp.float32),
             pltpu.VMEM((kv_heads, tall, 2 * HEAD_SIZE), jnp.float32),
             pltpu.VMEM((kv_heads, tall, 2 * HEAD_SIZE), jnp.float32),
-            pltpu.SemaphoreType.DMA((2 * kv_heads + 2,)),
-            pltpu.SemaphoreType.DMA((2, 2, kv_heads, n)),
-            pltpu.SemaphoreType.DMA((2, 2, kv_heads, n)),
+            pltpu.SemaphoreType.DMA((2 * kv_heads * n,)),
+            pltpu.SemaphoreType.DMA((2,)),
+            pltpu.SemaphoreType.DMA((2,)),
+            pltpu.SemaphoreType.REGULAR,
         ],
         compiler_params=pltpu.CompilerParams(
             collective_id=0, has_side_effects=True, vmem_limit_bytes=32 * 2**20

time: 23.8 us -> 23 us (0.966)
  Pallas kernels: 22.9 us -> 22.1 us
    pallas_call x1, Pallas kernels: 22.9 us -> 22.1 us  [shards(): pl.pallas_call(functools.partial(attend, n), out_shape=jax.ShapeDtypeStru...]
where the time goes in v2:
time: 23 us; the launch traced here: 22.9 us
  Pallas kernels  22.1 us (96%)
  local copies, waits for them, and re-layouts  0.8 us (3%)
    pallas_call x1, Pallas kernels, shards(): pl.pallas_call(functools.partial(attend, n), out_shape=jax.ShapeDtypeStru...  22.1 us
    unnamed x1, local copies, waits for them, and re-layouts  0.8 us

profile of v2, /device:TPU:0, one launch (start us, length us, event | category | flops | bytes accessed | tf_op | source)
XLA Modules:
  0.0 22.9 jit_solution(78603676598942241)
XLA Ops:
  0.0 22.1 %shard_map.46 = bf16[256,1024]{1,0:T(8,128)(2,1)S(1)} custom-call(s32[8]{0:T(128)} %order_hbm.1, bf16[256,1024]{1,0:T(8,128)(2,1)} %q_hbm.1, bf16[256,256]{1,0:T(8,128)(2,1)} %k_hbm.1, bf16[256,256]{1,0:T(8,128)(2,1)} %v_hbm.1), custom_call_target="tpu_custom_call" | custom-call | tf_op jit(solution)/shard_map/pallas_call | solution.py:262
  22.1 0.8 %copy.6 = bf16[256,1024]{1,0:T(8,128)(2,1)} copy(bf16[256,1024]{1,0:T(8,128)(2,1)S(1)} %shard_map.46) | data formatting | bytes 1048576

commit v3 on v2

--- a/solution.py
+++ b/solution.py
@@ -12,13 +12,15 @@
 MASKED = -1e30
 MESH = pl.DeviceIdType.MESH
 KEY, VALUE = 0, 1
-OWN, RELAYED = 0, 1
+SIDES = ("groups", "head")
+ROUTES = ((1, 0), (0, 1), (1, 1))
+OWN, RELAYED, DETOURED, PARTIAL = 0, 1, 2, 3
 
 
 def attend(
-    n, order_hbm, q_hbm, k_hbm, v_hbm, out_ref,
-    order_ref, q_ref, kv_ref, stack_ref, p_ref, top_ref, sum_ref, acc_ref,
-    chunk_sem, load_sem, send_sem, entered_sem,
+    n, sides, order_hbm, q_hbm, k_hbm, v_hbm, out_ref,
+    order_ref, q_ref, kv_ref, detour_ref, stack_ref, p_ref, top_ref, sum_ref, acc_ref,
+    chunk_sem, load_sem, send_sem, detour_sem, entered_sem,
 ):
     me = lax.axis_index("ctx")
     rows, q_cols = q_ref.shape
@@ -46,10 +48,9 @@
     ]
     load_order = pltpu.make_async_copy(order_hbm, order_ref, load_sem.at[0])
     load_q = pltpu.make_async_copy(q_hbm, q_ref, load_sem.at[1])
+    load_order.start()
     for load in loads:
         load.start()
-    load_q.start()
-    load_order.start()
 
     major = jnp.where(me < n // 2, -1, 1)
 
@@ -62,9 +63,36 @@
     def _():
         pl.semaphore_signal(barrier, inc=1, device_id={"ctx": me + 1}, device_id_type=MESH)
 
+    core = lax.axis_index("rep")
+
+    def on_line(route):
+        return (lax.axis_index(SIDES[0]) == route[0]) & (lax.axis_index(SIDES[1]) == route[1])
+
+    def via(route):
+        return {SIDES[0]: route[0], SIDES[1]: route[1], "rep": 1}
+
+    corner = on_line((0, 0)) & (core == 0)
+    source = corner & (me == n - 1)
+    spared = corner & (me == 1)
+    beside = [on_line(route) & (core == 1) & (me == n - 1) for route in ROUTES]
+    if sides:
+        @pl.when(corner & (me == 0))
+        def _():
+            for route in ROUTES:
+                pl.semaphore_signal(
+                    barrier, inc=1, device_id={"ctx": n - 1, **via(route)}, device_id_type=MESH
+                )
+
+        @pl.when(beside[0] | beside[1] | beside[2])
+        def _():
+            pl.semaphore_signal(
+                barrier, inc=1, device_id={"groups": 0, "head": 0, "rep": 0}, device_id_type=MESH
+            )
+
     @pl.when(me > 0)
     def _():
-        pl.semaphore_wait(barrier, 1)
+        helpers = jnp.where(source, len(ROUTES), jnp.where(beside[0] | beside[1] | beside[2], 1, 0))
+        pl.semaphore_wait(barrier, 1 + helpers if sides else 1)
         pl.semaphore_signal(entered_sem, inc=1, device_id={"ctx": me - 1}, device_id_type=MESH)
 
     def send(way, at, pool, count=None):
@@ -81,19 +109,71 @@
     def take(way, kind, head, step):
         send(-way, place(kind, head, me - way * step), RELAYED).wait_recv()
 
-    def arrive(way, kind, head, step):
+    half = rows // 2
+    pieces = [(KEY, 0), (KEY, half), (VALUE, 0)]
+
+    def far_part(kind, start):
+        return kv_ref.at[place(kind, kv_heads - 1, n - 1), pl.ds(start, half)]
+
+    def divert(i):
+        return pltpu.make_async_remote_copy(
+            src_ref=far_part(*pieces[i]),
+            dst_ref=detour_ref,
+            send_sem=send_sem.at[PARTIAL if pieces[i][0] == VALUE else DETOURED],
+            recv_sem=detour_sem,
+            device_id=via(ROUTES[i]),
+            device_id_type=MESH,
+        )
+
+    def rejoin(i):
+        return pltpu.make_async_remote_copy(
+            src_ref=detour_ref,
+            dst_ref=far_part(*pieces[i]),
+            send_sem=send_sem.at[DETOURED],
+            recv_sem=chunk_sem.at[place(pieces[i][0], kv_heads - 1, n - 1)],
+            device_id={"ctx": 0, "groups": 0, "head": 0, "rep": 0},
+            device_id_type=MESH,
+        )
+
+    def remainder():
+        return pltpu.make_async_remote_copy(
+            src_ref=far_part(VALUE, half),
+            dst_ref=far_part(VALUE, half),
+            send_sem=send_sem.at[PARTIAL],
+            recv_sem=chunk_sem.at[place(VALUE, kv_heads - 1, n - 1)],
+            device_id={"ctx": 0},
+            device_id_type=MESH,
+        )
+
+    def arrive(way, kind, head, step, leading):
         take(way, kind, head, step)
-
-        @pl.when(inside(me + way))
+        onward = inside(me + way)
+        if sides and leading and head == kv_heads - 1:
+            last = spared & (step == n - 2)
+            onward &= jnp.logical_not(last)
+            if kind == VALUE:
+                @pl.when(last)
+                def _():
+                    remainder().start()
+
+        @pl.when(onward)
         def _():
             send(way, place(kind, head, me - way * step), RELAYED).start()
 
     for load, (kind, head) in zip(loads, chunks):
         load.wait()
+        if kind == KEY and head == 0:
+            load_q.start()
 
         @pl.when(me > 0)
         def _():
             send(-1, place(kind, head, me), OWN).start()
+
+    if sides:
+        @pl.when(source)
+        def _():
+            for i in range(len(ROUTES)):
+                divert(i).start()
 
     @pl.when(me < n - 1)
     def _():
@@ -170,6 +250,13 @@
         acc_ref[head] = jnp.concatenate(stored(low[:, :HEAD_SIZE], high[:, :HEAD_SIZE]), axis=1)
         sum_ref[head] = jnp.concatenate(stored(low[:, HEAD_SIZE:], high[:, HEAD_SIZE:]), axis=1)
 
+    if sides:
+        for i in range(len(ROUTES)):
+            @pl.when(beside[i])
+            def _():
+                divert(i).wait_recv()
+                rejoin(i).start()
+
     def weigh(block, head):
         earlier = low_span(block) < low_span(me)
         key_low, key_high = low_high(KEY, block, head)
@@ -208,9 +295,9 @@
         for way in (major, -major):
             @pl.when(inside(me - way * step))
             def _():
-                arrive(way, KEY, head, step)
+                arrive(way, KEY, head, step, way is major)
                 weigh(me - way * step, head)
-                arrive(way, VALUE, head, step)
+                arrive(way, VALUE, head, step, way is major)
                 acc_ref[head] = gathered(me - way * step, head)
 
     def steps(step, carry):
@@ -219,6 +306,7 @@
         return carry
 
     lax.fori_loop(1, n - 1, steps, 0)
+
 
     def finish(head, total):
         result = (total * sum_ref[head]).astype(out_ref.dtype)
@@ -243,24 +331,44 @@
             sum_ref[head] = 1.0 / sum_ref[head]
             finish(head, acc_ref[head])
 
-    @pl.when((me > 0) & (me < n - 1))
+    if sides:
+        @pl.when(source)
+        def _():
+            send(1, 0, DETOURED, 1).wait_send()
+            divert(2).wait_send()
+
+        @pl.when(beside[0] | beside[1] | beside[2])
+        def _():
+            rejoin(0).wait_send()
+
+        @pl.when(spared)
+        def _():
+            send(1, 0, RELAYED, (n - 1) * per_block - 2).wait_send()
+            remainder().wait_send()
+
+    middle = (me > 0) & (me < n - 1)
+
+    @pl.when(middle & jnp.logical_not(spared) if sides else middle)
+    def _():
+        send(1, 0, RELAYED, (n - 1) * per_block).wait_send()
+
+    @pl.when(middle)
     def _():
         send(1, 0, OWN, 2 * per_block).wait_send()
-        send(1, 0, RELAYED, (n - 1) * per_block).wait_send()
-
-    @pl.when((me == 0) | (me == n - 1))
+
+    @pl.when(jnp.logical_not(middle))
     def _():
         send(1, 0, OWN, per_block).wait_send()
 
 
-def shards(n, queries, keys, values, span_order):
+def shards(n, sides, queries, keys, values, span_order):
     rows, q_cols = queries.shape
     span = rows // 2
     kv_heads = keys.shape[1] // HEAD_SIZE
     tall = q_cols // HEAD_SIZE // kv_heads * span
     inputs = [pltpu.with_memory_space_constraint(x, pltpu.HBM) for x in (span_order, queries, keys, values)]
     return pl.pallas_call(
-        functools.partial(attend, n),
+        functools.partial(attend, n, sides),
         out_shape=jax.ShapeDtypeStruct((rows, q_cols), jnp.bfloat16),
         in_specs=[pl.BlockSpec(memory_space=pltpu.HBM)] * 4,
         out_specs=pl.BlockSpec(memory_space=pltpu.VMEM),
@@ -268,6 +376,7 @@
             pltpu.SMEM(span_order.shape, jnp.int32),
             pltpu.VMEM((rows, q_cols), jnp.bfloat16),
             pltpu.VMEM((2 * kv_heads * n, rows, HEAD_SIZE), jnp.bfloat16),
+            pltpu.VMEM((rows // 2, HEAD_SIZE), jnp.bfloat16),
             pltpu.VMEM((kv_heads, 2, tall, HEAD_SIZE), jnp.bfloat16),
             pltpu.VMEM((kv_heads, tall, 2 * span), jnp.bfloat16),
             pltpu.VMEM((kv_heads, 2, tall, HEAD_SIZE), jnp.float32),
@@ -275,7 +384,8 @@
             pltpu.VMEM((kv_heads, tall, 2 * HEAD_SIZE), jnp.float32),
             pltpu.SemaphoreType.DMA((2 * kv_heads * n,)),
             pltpu.SemaphoreType.DMA((2,)),
-            pltpu.SemaphoreType.DMA((2,)),
+            pltpu.SemaphoreType.DMA((4,)),
+            pltpu.SemaphoreType.DMA,
             pltpu.SemaphoreType.REGULAR,
         ],
         compiler_params=pltpu.CompilerParams(
@@ -286,8 +396,10 @@
 
 def solution(mesh):
     split = P(("groups", "ctx"), ("head", "rep"))
+    n = mesh.shape["ctx"]
+    sides = n > 2 and min(mesh.shape[axis] for axis in SIDES + ("rep",)) > 1
     return jax.shard_map(
-        functools.partial(shards, mesh.shape["ctx"]),
+        functools.partial(shards, n, sides),
         mesh=mesh,
         in_specs=(split, split, split, P()),
         out_specs=split,

time: 23 us -> 21.8 us (0.948)
  Pallas kernels: 22.1 us -> 20.9 us
    pallas_call x1, Pallas kernels: 22.1 us -> 20.9 us  [shards(): pl.pallas_call(functools.partial(attend, n, sides), out_shape=jax.ShapeDt...]
where the time goes in v3:
time: 21.8 us; the launch traced here: 21.7 us
  Pallas kernels  20.9 us (96%)
  local copies, waits for them, and re-layouts  0.8 us (4%)
    pallas_call x1, Pallas kernels, shards(): pl.pallas_call(functools.partial(attend, n, sides), out_shape=jax.ShapeDt...  20.9 us
    unnamed x1, local copies, waits for them, and re-layouts  0.8 us

profile of v3, /device:TPU:0, one launch (start us, length us, event | category | flops | bytes accessed | tf_op | source)
XLA Modules:
  0.0 21.7 jit_solution(7147120771843319184)
XLA Ops:
  0.0 20.9 %shard_map.46 = bf16[256,1024]{1,0:T(8,128)(2,1)S(1)} custom-call(s32[8]{0:T(128)} %order_hbm.1, bf16[256,1024]{1,0:T(8,128)(2,1)} %q_hbm.1, bf16[256,256]{1,0:T(8,128)(2,1)} %k_hbm.1, bf16[256,256]{1,0:T(8,128)(2,1)} %v_hbm.1), custom_call_target="tpu_custom_call" | custom-call | tf_op jit(solution)/shard_map/pallas_call | solution.py:370
  20.9 0.8 %copy.6 = bf16[256,1024]{1,0:T(8,128)(2,1)} copy(bf16[256,1024]{1,0:T(8,128)(2,1)S(1)} %shard_map.46) | data formatting | bytes 1048576

commit v4 on v3

v4 whole, which is shorter than its diff:
```python
import functools
import math

import jax
import jax.numpy as jnp
from jax import lax
from jax.experimental import pallas as pl
from jax.experimental.pallas import tpu as pltpu
from jax.sharding import PartitionSpec as P

HEAD_SIZE = 128
MASKED = -1e30
MESH = pl.DeviceIdType.MESH
KEY, VALUE = 0, 1
OWN, RELAYED = 0, 1
SIDES = ("groups", "head")
ROUTES = ((1, 0), (0, 1), (1, 1), (0, 0))


def columns(head):
    return pl.ds(head * HEAD_SIZE, HEAD_SIZE)


def product(weights, values):
    return jnp.dot(weights, values, preferred_element_type=jnp.float32)


def attend(n, sides, *refs):
    order_hbm, q_hbm, k_hbm, v_hbm = refs[:4]
    (
        acc_out, sum_out, p_out, mix_out,
        order_ref, q_ref, kv_ref, detour_ref, stack_ref, top_ref,
        chunk_sem, load_sem, send_sem, detour_sem, entered_sem,
    ) = refs[-15:]
    done_out, p_ref, sum_ref, acc_ref = refs[4:-15] or (None,) * 4
    me = lax.axis_index("ctx")
    rows, q_cols = q_ref.shape
    span = rows // 2
    kv_heads = k_hbm.shape[1] // HEAD_SIZE
    per_block = 2 * kv_heads
    group = q_cols // HEAD_SIZE // kv_heads
    tall = group * span
    half = rows // 2
    exponent_scale = math.log2(math.e) / math.sqrt(HEAD_SIZE)
    chunks = [(kind, head) for head in range(kv_heads) for kind in (KEY, VALUE)]
    tops = range(kv_heads)
    accs = [acc_ref.at[h] for h in tops[:-1]] + [acc_out]
    sums = [sum_ref.at[h] for h in tops[:-1]] + [sum_out]
    weights_refs = [p_ref.at[h] for h in tops[:-1]] + [p_out]

    def part(kind, head, block, start=0, count=rows):
        at = (block * per_block + 2 * head + kind) * rows + start
        return pl.ds(pl.multiple_of(at, half), count)

    def landing(kind, head, block, device):
        slot = lax.rem(block - device - 1 + n, n)
        return chunk_sem.at[slot * per_block + 2 * head + kind]

    def load(kind, head, sem):
        return pltpu.make_async_copy(
            (k_hbm, v_hbm)[kind].at[:, columns(head)], kv_ref.at[part(kind, head, me)], load_sem.at[sem]
        )

    load_order = pltpu.make_async_copy(order_hbm, order_ref, load_sem.at[1])
    load_q = pltpu.make_async_copy(q_hbm, q_ref, load_sem.at[0])
    load(*chunks[0], 0).start()
    for chunk in chunks[1:]:
        load(*chunk, 1).start()

    major = jnp.where(me < n // 2, -1, 1)

    def inside(index):
        return (index >= 0) & (index < n)

    barrier = pltpu.get_barrier_semaphore()

    @pl.when(me < n - 1)
    def _():
        pl.semaphore_signal(barrier, inc=1, device_id={"ctx": me + 1}, device_id_type=MESH)

    core = lax.axis_index("rep")

    def on_line(route):
        return (lax.axis_index(SIDES[0]) == route[0]) & (lax.axis_index(SIDES[1]) == route[1])

    def via(route):
        return {SIDES[0]: route[0], SIDES[1]: route[1], "rep": 1}

    ways_round = list(zip(ROUTES, [
        (KEY, kv_heads - 1, 0), (KEY, kv_heads - 1, half), (VALUE, kv_heads - 1, 0), (VALUE, 0, 0)
    ]))[: 3 if kv_heads == 1 else 4]
    corner = on_line((0, 0)) & (core == 0)
    source = corner & (me == n - 1)
    spared = corner & (me == 1)
    beside = [on_line(route) & (core == 1) & (me == n - 1) for route, _ in ways_round]
    helper = functools.reduce(jnp.logical_or, beside)
    if sides:
        @pl.when(corner & (me == 0))
        def _():
            for route, _ in ways_round:
                pl.semaphore_signal(
                    barrier, inc=1, device_id={"ctx": n - 1, **via(route)}, device_id_type=MESH
                )

        @pl.when(helper)
        def _():
            pl.semaphore_signal(
                barrier, inc=1, device_id={"groups": 0, "head": 0, "rep": 0}, device_id_type=MESH
            )

    @pl.when(me > 0)
    def _():
        others = jnp.where(source, len(ways_round), jnp.where(helper, 1, 0))
        pl.semaphore_wait(barrier, 1 + others if sides else 1)
        pl.semaphore_signal(entered_sem, inc=1, device_id={"ctx": me - 1}, device_id_type=MESH)

    def send(way, kind, head, block, pool, start=0, count=rows):
        target = jnp.clip(me + way, 0, n - 1)
        return pltpu.make_async_remote_copy(
            src_ref=kv_ref.at[part(kind, head, block, start, count)],
            dst_ref=kv_ref.at[part(kind, head, block, start, count)],
            send_sem=send_sem.at[pool],
            recv_sem=landing(kind, head, block, target),
            device_id={"ctx": target},
            device_id_type=MESH,
        )

    def sent(pool, count):
        everything = kv_ref.at[pl.ds(0, count)]
        pltpu.make_async_remote_copy(
            src_ref=everything,
            dst_ref=everything,
            send_sem=send_sem.at[pool],
            recv_sem=detour_sem,
            device_id={"ctx": me},
            device_id_type=MESH,
        ).wait_send()

    def take(way, kind, head, step):
        block = me - way * step
        pltpu.make_async_remote_copy(
            src_ref=kv_ref.at[part(kind, head, block)],
            dst_ref=kv_ref.at[part(kind, head, block)],
            send_sem=send_sem.at[RELAYED],
            recv_sem=landing(kind, head, block, me),
            device_id={"ctx": me},
            device_id_type=MESH,
        ).wait_recv()

    def divert(route, piece):
        kind, head, start = piece
        return pltpu.make_async_remote_copy(
            src_ref=kv_ref.at[part(kind, head, n - 1, start, half)],
            dst_ref=detour_ref,
            send_sem=send_sem.at[OWN],
            recv_sem=detour_sem,
            device_id=via(route),
            device_id_type=MESH,
        )

    def rejoin(piece):
        kind, head, start = piece
        return pltpu.make_async_remote_copy(
            src_ref=detour_ref,
            dst_ref=kv_ref.at[part(kind, head, n - 1, start, half)],
            send_sem=send_sem.at[OWN],
            recv_sem=landing(kind, head, n - 1, 0),
            device_id={"ctx": 0, "groups": 0, "head": 0, "rep": 0},
            device_id_type=MESH,
        )

    def arrive(way, kind, head, step, leading):
        take(way, kind, head, step)
        onward = inside(me + way)
        gone = [start for _, (*chunk, start) in ways_round if chunk == [kind, head]]
        if sides and leading and gone:
            last = spared & (step == n - 2)
            onward &= jnp.logical_not(last)
            if len(gone) == 1:
                @pl.when(last)
                def _():
                    send(-1, kind, head, me + step, RELAYED, half, half).start()

        @pl.when(onward)
        def _():
            send(way, kind, head, me - way * step, RELAYED).start()

    def send_own(way, kind, head):
        send(way, kind, head, me, OWN).start()

    load(*chunks[0], 0).wait()
    load_q.start()

    @pl.when(me > 0)
    def _():
        send_own(-1, *chunks[0])

    rest = kv_ref.at[part(VALUE, 0, me, 0, (per_block - 1) * rows)]
    pltpu.make_async_copy(rest, rest, load_sem.at[1]).wait()
    load_order.start()

    @pl.when(me > 0)
    def _():
        for chunk in chunks[1:]:
            send_own(-1, *chunk)

    if sides:
        @pl.when(source)
        def _():
            for route, piece in ways_round:
                divert(route, piece).start()

    @pl.when(me < n - 1)
    def _():
        pl.semaphore_wait(entered_sem, 1)
        for chunk in chunks:
            send_own(1, *chunk)

    load_q.wait()
    load_order.wait()

    def low_first(block):
        return order_ref[2 * block] < order_ref[2 * block + 1]

    def low_span(block):
        return jnp.minimum(order_ref[2 * block], order_ref[2 * block + 1])

    def low_high(kind, block, head):
        first = kv_ref[part(kind, head, block, 0, span)]
        second = kv_ref[part(kind, head, block, span, span)]
        swap = low_first(block)
        return jnp.where(swap, first, second), jnp.where(swap, second, first)

    def score(queries, keys):
        return lax.dot_general(
            queries, keys, (((1,), (1,)), ((), ())), preferred_element_type=jnp.float32
        )

    def peak(scores):
        return jnp.broadcast_to(jnp.max(scores, axis=1, keepdims=True), (tall, HEAD_SIZE))

    def weights_of(scores, top):
        return jnp.exp2((scores - top) * exponent_scale).astype(jnp.bfloat16)

    mine_first = low_first(me)

    def stored(low, high):
        return jnp.where(mine_first, low, high), jnp.where(mine_first, high, low)

    def mixer(earlier, low, high):
        none = jnp.zeros_like(low)
        to_low = jnp.concatenate([none, jnp.where(earlier, low, none)], axis=0)
        to_high = jnp.concatenate([low, jnp.where(earlier, none, high)], axis=0)
        return jnp.concatenate(stored(to_low, to_high), axis=1)

    for head in range(kv_heads):
        for member in range(group):
            column = columns(head * group + member)
            low, high = stored(q_ref[:span, column], q_ref[span:, column])
            stack_ref[head, 0, member * span : (member + 1) * span] = low
            stack_ref[head, 1, member * span : (member + 1) * span] = high

    row = lax.rem(lax.broadcasted_iota(jnp.int32, (tall, span), 0), span)
    bias = jnp.where(lax.broadcasted_iota(jnp.int32, (tall, span), 1) <= row, 0.0, MASKED)
    ones = jnp.ones((span, HEAD_SIZE), jnp.bfloat16)
    for head in range(kv_heads):
        key_low, key_high = low_high(KEY, me, head)
        value_low, value_high = low_high(VALUE, me, head)
        low = score(stack_ref[head, 0], key_low) + bias
        low_top = peak(low)
        top_ref[head, 0] = low_top
        low = weights_of(low, low_top)
        cross = score(stack_ref[head, 1], key_low)
        high = score(stack_ref[head, 1], key_high) + bias
        high_top = jnp.maximum(peak(cross), peak(high))
        top_ref[head, 1] = high_top
        high = jnp.concatenate([weights_of(cross, high_top), weights_of(high, high_top)], axis=1)
        low = product(low, jnp.concatenate([value_low, ones], axis=1))
        high = product(high, jnp.concatenate(
            [jnp.concatenate([value_low, value_high], axis=0), jnp.concatenate([ones, ones], axis=0)], axis=1
        ))
        accs[head][...] = jnp.concatenate(stored(low[:, :HEAD_SIZE], high[:, :HEAD_SIZE]), axis=1)
        sums[head][...] = jnp.concatenate(stored(low[:, HEAD_SIZE:], high[:, HEAD_SIZE:]), axis=1)

    if sides:
        for (route, piece), here in zip(ways_round, beside):
            @pl.when(here)
            def _():
                divert(route, piece).wait_recv()
                rejoin(piece).start()

    def weigh(block, head):
        earlier = low_span(block) < low_span(me)
        key_low, key_high = low_high(KEY, block, head)
        cross = score(stack_ref[head, 1], key_low)
        other = score(
            jnp.where(earlier, stack_ref[head, 0], stack_ref[head, 1]),
            jnp.where(earlier, key_low, key_high),
        )
        other_top = peak(other)
        old_low, old_high = top_ref[head, 0], top_ref[head, 1]
        low_top = jnp.maximum(old_low, jnp.where(earlier, other_top, MASKED))
        high_top = jnp.maximum(
            jnp.maximum(old_high, peak(cross)), jnp.where(earlier, MASKED, other_top)
        )
        top_ref[head, 0] = low_top
        top_ref[head, 1] = high_top
        weights = jnp.concatenate(
            [weights_of(cross, high_top), weights_of(other, jnp.where(earlier, low_top, high_top))], axis=1
        )
        weights_refs[head][...] = weights
        fade = jnp.concatenate(
            stored(
                jnp.exp2((old_low - low_top) * exponent_scale),
                jnp.exp2((old_high - high_top) * exponent_scale),
            ),
            axis=1,
        )
        accs[head][...] *= fade
        sums[head][...] = sums[head][...] * fade + product(weights, mixer(earlier, ones, ones))

    def mixed(block, head):
        return mixer(low_span(block) < low_span(me), *low_high(VALUE, block, head))

    def gathered(block, head):
        return accs[head][...] + product(weights_refs[head][...], mixed(block, head))

    def turn(step, head):
        for way in (major, -major):
            @pl.when(inside(me - way * step))
            def _():
                arrive(way, KEY, head, step, way is major)
                weigh(me - way * step, head)
                arrive(way, VALUE, head, step, way is major)
                accs[head][...] = gathered(me - way * step, head)

    def steps(step, carry):
        for head in range(kv_heads):
            turn(step, head)
        return carry

    lax.fori_loop(1, n - 1, steps, 0)

    def finish(head, total):
        place(done_out, head * group, span, (total * sums[head][...]).astype(jnp.bfloat16))

    last = me - major * (n - 1)
    for head in range(kv_heads - 1):
        @pl.when(inside(last))
        def _():
            take(major, KEY, head, n - 1)
            weigh(last, head)
            sums[head][...] = 1.0 / sums[head][...]
            take(major, VALUE, head, n - 1)
            finish(head, gathered(last, head))

        @pl.when(jnp.logical_not(inside(last)))
        def _():
            sums[head][...] = 1.0 / sums[head][...]
            finish(head, accs[head][...])

    @pl.when(inside(last))
    def _():
        take(major, KEY, kv_heads - 1, n - 1)
        weigh(last, kv_heads - 1)

    sum_out[...] = 1.0 / sum_out[...]

    middle = (me > 0) & (me < n - 1)

    @pl.when(middle)
    def _():
        sent(OWN, 2 * per_block * rows)
        mix_out[...] = jnp.zeros_like(mix_out)

    @pl.when(middle & jnp.logical_not(spared) if sides else middle)
    def _():
        sent(RELAYED, (n - 1) * per_block * rows)

    if sides:
        @pl.when(spared)
        def _():
            sent(RELAYED, (n - 1) * per_block * rows - len(ways_round) * half)

        @pl.when(source)
        def _():
            sent(OWN, per_block * rows + len(ways_round) * half)

        @pl.when(helper)
        def _():
            sent(OWN, per_block * rows + half)

    plain = jnp.logical_not(middle)
    if sides:
        plain &= jnp.logical_not(source | helper)

    @pl.when(plain)
    def _():
        sent(OWN, per_block * rows)

    @pl.when(inside(last))
    def _():
        take(major, VALUE, kv_heads - 1, n - 1)
        mix_out[...] = mixed(last, kv_heads - 1)


def place(ref, first, span, result):
    for member in range(result.shape[0] // span):
        block = result[member * span : (member + 1) * span]
        ref[:span, columns(first + member)] = block[:, :HEAD_SIZE]
        ref[span:, columns(first + member)] = block[:, HEAD_SIZE:]


def conclude(acc_ref, sum_ref, p_ref, mix_ref, *refs):
    out_hbm, stage_ref, sem = refs[-3:]
    done_refs = refs[:-3]
    span = stage_ref.shape[0] // 2
    group = acc_ref.shape[0] // span
    before = out_hbm.shape[1] // HEAD_SIZE - group
    for done_ref in done_refs:
        pltpu.make_async_copy(done_ref, out_hbm.at[:, pl.ds(0, before * HEAD_SIZE)], sem).start()
    for member in range(group):
        part = slice(member * span, (member + 1) * span)
        result = (acc_ref[part] + product(p_ref[part], mix_ref[...])) * sum_ref[part]
        place(stage_ref, member, span, result.astype(stage_ref.dtype))
        pltpu.make_async_copy(
            stage_ref.at[:, columns(member)], out_hbm.at[:, columns(before + member)], sem
        ).start()
    pltpu.make_async_copy(out_hbm, out_hbm, sem).wait()


def shards(n, sides, queries, keys, values, span_order):
    rows, q_cols = queries.shape
    span = rows // 2
    kv_heads = keys.shape[1] // HEAD_SIZE
    group = q_cols // HEAD_SIZE // kv_heads
    tall = group * span
    wide = 2 * HEAD_SIZE
    vmem = pl.BlockSpec(memory_space=pltpu.VMEM)
    inputs = [pltpu.with_memory_space_constraint(x, pltpu.HBM) for x in (span_order, queries, keys, values)]
    early = kv_heads - 1
    done = [jax.ShapeDtypeStruct((rows, early * group * HEAD_SIZE), jnp.bfloat16)] if early else []
    pending = [
        jax.ShapeDtypeStruct((tall, wide), jnp.float32),
        jax.ShapeDtypeStruct((tall, wide), jnp.float32),
        jax.ShapeDtypeStruct((tall, 2 * span), jnp.bfloat16),
        jax.ShapeDtypeStruct((2 * span, wide), jnp.bfloat16),
    ]
    early_scratch = [
        pltpu.VMEM((early, tall, 2 * span), jnp.bfloat16),
        pltpu.VMEM((early, tall, wide), jnp.float32),
        pltpu.VMEM((early, tall, wide), jnp.float32),
    ] if early else []

    def kernel(*refs):
        outs = len(done) + len(pending)
        ins, out, scratch = refs[:4], refs[4 : 4 + outs], refs[4 + outs :]
        extra = out[: len(done)] + scratch[: len(early_scratch)]
        attend(n, sides, *ins, *extra, *out[len(done) :], *scratch[len(early_scratch) :])

    results = pl.pallas_call(
        kernel,
        out_shape=done + pending,
        in_specs=[pl.BlockSpec(memory_space=pltpu.HBM)] * 4,
        out_specs=[vmem] * (len(done) + len(pending)),
        scratch_shapes=early_scratch + [
            pltpu.SMEM(span_order.shape, jnp.int32),
            pltpu.VMEM((rows, q_cols), jnp.bfloat16),
            pltpu.VMEM((2 * kv_heads * n * rows, HEAD_SIZE), jnp.bfloat16),
            pltpu.VMEM((rows // 2, HEAD_SIZE), jnp.bfloat16),
            pltpu.VMEM((kv_heads, 2, tall, HEAD_SIZE), jnp.bfloat16),
            pltpu.VMEM((kv_heads, 2, tall, HEAD_SIZE), jnp.float32),
            pltpu.SemaphoreType.DMA((2 * kv_heads * (n - 1),)),
            pltpu.SemaphoreType.DMA((2,)),
            pltpu.SemaphoreType.DMA((2,)),
            pltpu.SemaphoreType.DMA,
            pltpu.SemaphoreType.REGULAR,
        ],
        compiler_params=pltpu.CompilerParams(
            collective_id=0, has_side_effects=True, vmem_limit_bytes=32 * 2**20
        ),
    )(*inputs)
    operands = results[len(done) :] + results[: len(done)]
    return pl.pallas_call(
        conclude,
        out_shape=jax.ShapeDtypeStruct((rows, q_cols), jnp.bfloat16),
        in_specs=[vmem] * len(operands),
        out_specs=pl.BlockSpec(memory_space=pltpu.HBM),
        scratch_shapes=[
            pltpu.VMEM((rows, group * HEAD_SIZE), jnp.bfloat16),
            pltpu.SemaphoreType.DMA,
        ],
        compiler_params=pltpu.CompilerParams(vmem_limit_bytes=16 * 2**20),
    )(*operands)


def solution(mesh):
    split = P(("groups", "ctx"), ("head", "rep"))
    n = mesh.shape["ctx"]
    sides = n > 2 and min(mesh.shape[axis] for axis in SIDES + ("rep",)) > 1
    return jax.shard_map(
        functools.partial(shards, n, sides),
        mesh=mesh,
        in_specs=(split, split, split, P()),
        out_specs=split,
        check_vma=False,
    )
```

time: 21.8 us -> 21.6 us (level); the launches traced: 21.7 us -> 21.2 us
  local copies, waits for them, and re-layouts: 0.8 us -> 0 us
  Pallas kernels: 20.9 us -> 21.2 us
    unnamed x1 -> x0, local copies, waits for them, and re-layouts: 0.8 us -> none
    pallas_call x1 -> x2, Pallas kernels: 20.9 us -> 21.2 us  [the longest x1 20.2 us: shards(): pl.pallas_call(kernel, out_shape=done + pending, in_specs=[pl.BlockSpec(m...]
where the time goes in v4:
time: 21.6 us; the launch traced here: 21.2 us
  Pallas kernels  21.2 us (98%)
    pallas_call x1, Pallas kernels, shards(): pl.pallas_call(kernel, out_shape=done + pending, in_specs=[pl.BlockSpec(m...  20.2 us
    pallas_call x1, Pallas kernels, shards(): pl.pallas_call(conclude, out_shape=jax.ShapeDtypeStruct((rows, q_cols), j...  0.9 us

profile of v4, /device:TPU:0, one launch (start us, length us, event | category | flops | bytes accessed | tf_op | source)
XLA Modules:
  0.0 21.2 jit_solution(2339671815719357891)
XLA Ops:
  0.0 20.2 %shard_map.46 = (bf16[256,512]{1,0:T(8,128)(2,1)S(1)}, f32[512,256]{1,0:T(8,128)S(1)}, f32[512,256]{1,0:T(8,128)S(1)}, bf16[512,256]{1,0:T(8,128)(2,1)S(1)}, bf16[256,256]{1,0:T(8,128)(2,1)S(1)}) custom-call(s32[8]{0:T(128)} %refs_0_.1, bf16[256,1024]{1,0:T(8,128)(2,1)} %refs_1_.1, bf16[256,256]{1,0:T(8,128)(2,1)} %refs_2_.1, bf16[256,256]{1,0:T(8,128)(2,1)} %refs_3_.1), custom_call_target="tpu_custom_call" | custom-call | tf_op jit(solution)/shard_map/pallas_call | solution.py:461
  20.3 0.9 %shard_map.47 = bf16[256,1024]{1,0:T(8,128)(2,1)} custom-call(f32[512,256]{1,0:T(8,128)S(1)} %get-tuple-element.10.acc_ref, f32[512,256]{1,0:T(8,128)S(1)} %get-tuple-element.11.sum_ref, bf16[512,256]{1,0:T(8,128)(2,1)S(1)} %get-tuple-element.12.p_ref, bf16[256,256]{1,0:T(8,128)(2,1)S(1)} %get-tuple-element.13.mix_ref, ...), custom_call_target="tpu_custom_call" | custom-call | tf_op jit(solution)/shard_map/pallas_call | solution.py:484

commit v5 on v4

--- a/solution.py
+++ b/solution.py
@@ -12,6 +12,7 @@
 MASKED = -1e30
 MESH = pl.DeviceIdType.MESH
 KEY, VALUE = 0, 1
+DIRECT = 1
 OWN, RELAYED = 0, 1
 SIDES = ("groups", "head")
 ROUTES = ((1, 0), (0, 1), (1, 1), (0, 0))
@@ -185,15 +186,26 @@
         def _():
             send(way, kind, head, me - way * step, RELAYED).start()
 
+    def send_first(kind, head):
+        return pltpu.make_async_remote_copy(
+            src_ref=(k_hbm, v_hbm)[kind].at[:, columns(head)],
+            dst_ref=kv_ref.at[part(kind, head, me)],
+            send_sem=send_sem.at[OWN],
+            recv_sem=landing(kind, head, me, jnp.maximum(me - 1, 0)),
+            device_id={"ctx": jnp.maximum(me - 1, 0)},
+            device_id_type=MESH,
+        )
+
     def send_own(way, kind, head):
         send(way, kind, head, me, OWN).start()
 
+    @pl.when(me > 0)
+    def _():
+        for chunk in chunks[:DIRECT]:
+            send_first(*chunk).start()
+
     load(*chunks[0], 0).wait()
     load_q.start()
-
-    @pl.when(me > 0)
-    def _():
-        send_own(-1, *chunks[0])
 
     rest = kv_ref.at[part(VALUE, 0, me, 0, (per_block - 1) * rows)]
     pltpu.make_async_copy(rest, rest, load_sem.at[1]).wait()
@@ -201,7 +213,7 @@
 
     @pl.when(me > 0)
     def _():
-        for chunk in chunks[1:]:
+        for chunk in chunks[DIRECT:]:
             send_own(-1, *chunk)
 
     if sides:

time: 21.6 us -> 21.1 us (0.977)
  Pallas kernels: 21.2 us -> 20.8 us
    pallas_call x1, Pallas kernels: 20.2 us -> 19.9 us  [shards(): pl.pallas_call(kernel, out_shape=done + pending, in_specs=[pl.BlockSpec(m...]
where the time goes in v5:
time: 21.1 us; the launch traced here: 20.8 us
  Pallas kernels  20.8 us (99%)
    pallas_call x1, Pallas kernels, shards(): pl.pallas_call(kernel, out_shape=done + pending, in_specs=[pl.BlockSpec(m...  19.9 us
    pallas_call x1, Pallas kernels, shards(): pl.pallas_call(conclude, out_shape=jax.ShapeDtypeStruct((rows, q_cols), j...  0.9 us

profile of v5, /device:TPU:0, one launch (start us, length us, event | category | flops | bytes accessed | tf_op | source)
XLA Modules:
  0.0 20.8 jit_solution(4391352921827351789)
XLA Ops:
  0.0 19.9 %shard_map.46 = (bf16[256,512]{1,0:T(8,128)(2,1)S(1)}, f32[512,256]{1,0:T(8,128)S(1)}, f32[512,256]{1,0:T(8,128)S(1)}, bf16[512,256]{1,0:T(8,128)(2,1)S(1)}, bf16[256,256]{1,0:T(8,128)(2,1)S(1)}) custom-call(s32[8]{0:T(128)} %refs_0_.1, bf16[256,1024]{1,0:T(8,128)(2,1)} %refs_1_.1, bf16[256,256]{1,0:T(8,128)(2,1)} %refs_2_.1, bf16[256,256]{1,0:T(8,128)(2,1)} %refs_3_.1), custom_call_target="tpu_custom_call" | custom-call | tf_op jit(solution)/shard_map/pallas_call | solution.py:473
  19.9 0.9 %shard_map.47 = bf16[256,1024]{1,0:T(8,128)(2,1)} custom-call(f32[512,256]{1,0:T(8,128)S(1)} %get-tuple-element.10.acc_ref, f32[512,256]{1,0:T(8,128)S(1)} %get-tuple-element.11.sum_ref, bf16[512,256]{1,0:T(8,128)(2,1)S(1)} %get-tuple-element.12.p_ref, bf16[256,256]{1,0:T(8,128)(2,1)S(1)} %get-tuple-element.13.mix_ref, ...), custom_call_target="tpu_custom_call" | custom-call | tf_op jit(solution)/shard_map/pallas_call | solution.py:496

commit v6 on v5

--- a/solution.py
+++ b/solution.py
@@ -13,7 +13,6 @@
 MESH = pl.DeviceIdType.MESH
 KEY, VALUE = 0, 1
 DIRECT = 1
-OWN, RELAYED = 0, 1
 SIDES = ("groups", "head")
 ROUTES = ((1, 0), (0, 1), (1, 1), (0, 0))
 
@@ -51,7 +50,7 @@
 
     def part(kind, head, block, start=0, count=rows):
         at = (block * per_block + 2 * head + kind) * rows + start
-        return pl.ds(pl.multiple_of(at, half), count)
+        return pl.ds(pl.multiple_of(at, 16), count)
 
     def landing(kind, head, block, device):
         slot = lax.rem(block - device - 1 + n, n)
@@ -87,9 +86,16 @@
     def via(route):
         return {SIDES[0]: route[0], SIDES[1]: route[1], "rep": 1}
 
-    ways_round = list(zip(ROUTES, [
-        (KEY, kv_heads - 1, 0), (KEY, kv_heads - 1, half), (VALUE, kv_heads - 1, 0), (VALUE, 0, 0)
-    ]))[: 3 if kv_heads == 1 else 4]
+    end = kv_heads - 1
+    wide = rows * 7 // 16
+    ways_round = [
+        (ROUTES[0], [(KEY, end, 0, wide)]),
+        (ROUTES[1], [(KEY, end, wide, wide)]),
+        (ROUTES[2], [(KEY, end, 2 * wide, rows - 2 * wide), (VALUE, end, 0, 3 * half // 4)]),
+    ]
+    if kv_heads > 1:
+        ways_round.append((ROUTES[3], [(VALUE, 0, 0, half)]))
+    loads_round = [sum(count for *_, count in parts) for _, parts in ways_round]
     corner = on_line((0, 0)) & (core == 0)
     source = corner & (me == n - 1)
     spared = corner & (me == 1)
@@ -115,23 +121,23 @@
         pl.semaphore_wait(barrier, 1 + others if sides else 1)
         pl.semaphore_signal(entered_sem, inc=1, device_id={"ctx": me - 1}, device_id_type=MESH)
 
-    def send(way, kind, head, block, pool, start=0, count=rows):
+    def send(way, kind, head, block, start=0, count=rows):
         target = jnp.clip(me + way, 0, n - 1)
         return pltpu.make_async_remote_copy(
             src_ref=kv_ref.at[part(kind, head, block, start, count)],
             dst_ref=kv_ref.at[part(kind, head, block, start, count)],
-            send_sem=send_sem.at[pool],
+            send_sem=send_sem,
             recv_sem=landing(kind, head, block, target),
             device_id={"ctx": target},
             device_id_type=MESH,
         )
 
-    def sent(pool, count):
+    def sent(count):
         everything = kv_ref.at[pl.ds(0, count)]
         pltpu.make_async_remote_copy(
             src_ref=everything,
             dst_ref=everything,
-            send_sem=send_sem.at[pool],
+            send_sem=send_sem,
             recv_sem=detour_sem,
             device_id={"ctx": me},
             device_id_type=MESH,
@@ -142,62 +148,71 @@
         pltpu.make_async_remote_copy(
             src_ref=kv_ref.at[part(kind, head, block)],
             dst_ref=kv_ref.at[part(kind, head, block)],
-            send_sem=send_sem.at[RELAYED],
+            send_sem=send_sem,
             recv_sem=landing(kind, head, block, me),
             device_id={"ctx": me},
             device_id_type=MESH,
         ).wait_recv()
 
-    def divert(route, piece):
-        kind, head, start = piece
-        return pltpu.make_async_remote_copy(
-            src_ref=kv_ref.at[part(kind, head, n - 1, start, half)],
-            dst_ref=detour_ref,
-            send_sem=send_sem.at[OWN],
-            recv_sem=detour_sem,
-            device_id=via(route),
-            device_id_type=MESH,
-        )
-
-    def rejoin(piece):
-        kind, head, start = piece
-        return pltpu.make_async_remote_copy(
-            src_ref=detour_ref,
-            dst_ref=kv_ref.at[part(kind, head, n - 1, start, half)],
-            send_sem=send_sem.at[OWN],
-            recv_sem=landing(kind, head, n - 1, 0),
-            device_id={"ctx": 0, "groups": 0, "head": 0, "rep": 0},
-            device_id_type=MESH,
-        )
+    def divert(route, parts):
+        staged = 0
+        for kind, head, start, count in parts:
+            pltpu.make_async_remote_copy(
+                src_ref=kv_ref.at[part(kind, head, n - 1, start, count)],
+                dst_ref=detour_ref.at[pl.ds(staged, count)],
+                send_sem=send_sem,
+                recv_sem=detour_sem,
+                device_id=via(route),
+                device_id_type=MESH,
+            ).start()
+            staged += count
+
+    def rejoin(parts):
+        staged = sum(count for *_, count in parts)
+        whole = detour_ref.at[pl.ds(0, staged)]
+        pltpu.make_async_copy(whole, whole, detour_sem).wait()
+        staged = 0
+        for kind, head, start, count in parts:
+            pltpu.make_async_remote_copy(
+                src_ref=detour_ref.at[pl.ds(staged, count)],
+                dst_ref=kv_ref.at[part(kind, head, n - 1, start, count)],
+                send_sem=send_sem,
+                recv_sem=landing(kind, head, n - 1, 0),
+                device_id={"ctx": 0, "groups": 0, "head": 0, "rep": 0},
+                device_id_type=MESH,
+            ).start()
+            staged += count
 
     def arrive(way, kind, head, step, leading):
         take(way, kind, head, step)
         onward = inside(me + way)
-        gone = [start for _, (*chunk, start) in ways_round if chunk == [kind, head]]
+        gone = sum(
+            count for _, parts in ways_round for *chunk, _, count in parts if chunk == [kind, head]
+        )
         if sides and leading and gone:
             last = spared & (step == n - 2)
             onward &= jnp.logical_not(last)
-            if len(gone) == 1:
+            if gone < rows:
                 @pl.when(last)
                 def _():
-                    send(-1, kind, head, me + step, RELAYED, half, half).start()
+                    send(-1, kind, head, me + step, gone, rows - gone).start()
 
         @pl.when(onward)
         def _():
-            send(way, kind, head, me - way * step, RELAYED).start()
+            send(way, kind, head, me - way * step).start()
 
     def send_first(kind, head):
         return pltpu.make_async_remote_copy(
             src_ref=(k_hbm, v_hbm)[kind].at[:, columns(head)],
             dst_ref=kv_ref.at[part(kind, head, me)],
-            send_sem=send_sem.at[OWN],
+            send_sem=send_sem,
             recv_sem=landing(kind, head, me, jnp.maximum(me - 1, 0)),
             device_id={"ctx": jnp.maximum(me - 1, 0)},
             device_id_type=MESH,
         )
 
     def send_own(way, kind, head):
-        send(way, kind, head, me, OWN).start()
+        send(way, kind, head, me).start()
 
     @pl.when(me > 0)
     def _():
@@ -219,8 +234,8 @@
     if sides:
         @pl.when(source)
         def _():
-            for route, piece in ways_round:
-                divert(route, piece).start()
+            for route, parts in ways_round:
+                divert(route, parts)
 
     @pl.when(me < n - 1)
     def _():
@@ -295,11 +310,10 @@
         sums[head][...] = jnp.concatenate(stored(low[:, HEAD_SIZE:], high[:, HEAD_SIZE:]), axis=1)
 
     if sides:
-        for (route, piece), here in zip(ways_round, beside):
+        for (_, parts), here in zip(ways_round, beside):
             @pl.when(here)
             def _():
-                divert(route, piece).wait_recv()
-                rejoin(piece).start()
+                rejoin(parts)
 
     def weigh(block, head):
         earlier = low_span(block) < low_span(me)
@@ -382,33 +396,32 @@
 
     @pl.when(middle)
     def _():
-        sent(OWN, 2 * per_block * rows)
         mix_out[...] = jnp.zeros_like(mix_out)
 
     @pl.when(middle & jnp.logical_not(spared) if sides else middle)
     def _():
-        sent(RELAYED, (n - 1) * per_block * rows)
-
+        sent((n + 1) * per_block * rows)
+
+    plain = jnp.logical_not(middle)
     if sides:
         @pl.when(spared)
         def _():
-            sent(RELAYED, (n - 1) * per_block * rows - len(ways_round) * half)
+            sent((n + 1) * per_block * rows - sum(loads_round))
 
         @pl.when(source)
         def _():
-            sent(OWN, per_block * rows + len(ways_round) * half)
-
-        @pl.when(helper)
-        def _():
-            sent(OWN, per_block * rows + half)
-
-    plain = jnp.logical_not(middle)
-    if sides:
+            sent(per_block * rows + sum(loads_round))
+
+        for count, here in zip(loads_round, beside):
+            @pl.when(here)
+            def _():
+                sent(per_block * rows + count)
+
         plain &= jnp.logical_not(source | helper)
 
     @pl.when(plain)
     def _():
-        sent(OWN, per_block * rows)
+        sent(per_block * rows)
 
     @pl.when(inside(last))
     def _():
@@ -478,13 +491,13 @@
         scratch_shapes=early_scratch + [
             pltpu.SMEM(span_order.shape, jnp.int32),
             pltpu.VMEM((rows, q_cols), jnp.bfloat16),
-            pltpu.VMEM((2 * kv_heads * n * rows, HEAD_SIZE), jnp.bfloat16),
+            pltpu.VMEM((2 * kv_heads * (n + 1) * rows, HEAD_SIZE), jnp.bfloat16),
             pltpu.VMEM((rows // 2, HEAD_SIZE), jnp.bfloat16),
             pltpu.VMEM((kv_heads, 2, tall, HEAD_SIZE), jnp.bfloat16),
             pltpu.VMEM((kv_heads, 2, tall, HEAD_SIZE), jnp.float32),
             pltpu.SemaphoreType.DMA((2 * kv_heads * (n - 1),)),
             pltpu.SemaphoreType.DMA((2,)),
-            pltpu.SemaphoreType.DMA((2,)),
+            pltpu.SemaphoreType.DMA,
             pltpu.SemaphoreType.DMA,
             pltpu.SemaphoreType.REGULAR,
         ],
@@ -509,7 +522,7 @@
 def solution(mesh):
     split = P(("groups", "ctx"), ("head", "rep"))
     n = mesh.shape["ctx"]
-    sides = n > 2 and min(mesh.shape[axis] for axis in SIDES + ("rep",)) > 1
+    sides = n > 3 and min(mesh.shape[axis] for axis in SIDES + ("rep",)) > 1
     return jax.shard_map(
         functools.partial(shards, n, sides),
         mesh=mesh,

time: 21.1 us -> 21.2 us (level)
  no operation moved by 1% of the time
where the time goes in v6:
time: 21.2 us; the launch traced here: 21 us
  Pallas kernels  21 us (99%)
    pallas_call x1, Pallas kernels, shards(): pl.pallas_call(kernel, out_shape=done + pending, in_specs=[pl.BlockSpec(m...  20.1 us
    pallas_call x1, Pallas kernels, shards(): pl.pallas_call(conclude, out_shape=jax.ShapeDtypeStruct((rows, q_cols), j...  0.9 us

profile of v6, /device:TPU:0, one launch (start us, length us, event | category | flops | bytes accessed | tf_op | source)
XLA Modules:
  0.0 21.0 jit_solution(1909621691566637003)
XLA Ops:
  0.0 20.1 %shard_map.46 = (bf16[256,512]{1,0:T(8,128)(2,1)S(1)}, f32[512,256]{1,0:T(8,128)S(1)}, f32[512,256]{1,0:T(8,128)S(1)}, bf16[512,256]{1,0:T(8,128)(2,1)S(1)}, bf16[256,256]{1,0:T(8,128)(2,1)S(1)}) custom-call(s32[8]{0:T(128)} %refs_0_.1, bf16[256,1024]{1,0:T(8,128)(2,1)} %refs_1_.1, bf16[256,256]{1,0:T(8,128)(2,1)} %refs_2_.1, bf16[256,256]{1,0:T(8,128)(2,1)} %refs_3_.1), custom_call_target="tpu_custom_call" | custom-call | tf_op jit(solution)/shard_map/pallas_call | solution.py:486
  20.1 0.9 %shard_map.47 = bf16[256,1024]{1,0:T(8,128)(2,1)} custom-call(f32[512,256]{1,0:T(8,128)S(1)} %get-tuple-element.10.acc_ref, f32[512,256]{1,0:T(8,128)S(1)} %get-tuple-element.11.sum_ref, bf16[512,256]{1,0:T(8,128)(2,1)S(1)} %get-tuple-element.12.p_ref, bf16[256,256]{1,0:T(8,128)(2,1)S(1)} %get-tuple-element.13.mix_ref, ...), custom_call_target="tpu_custom_call" | custom-call | tf_op jit(solution)/shard_map/pallas_call | solution.py:509

commit v7 on v6

--- a/solution.py
+++ b/solution.py
@@ -87,11 +87,11 @@
         return {SIDES[0]: route[0], SIDES[1]: route[1], "rep": 1}
 
     end = kv_heads - 1
-    wide = rows * 7 // 16
+    wide = half
     ways_round = [
         (ROUTES[0], [(KEY, end, 0, wide)]),
         (ROUTES[1], [(KEY, end, wide, wide)]),
-        (ROUTES[2], [(KEY, end, 2 * wide, rows - 2 * wide), (VALUE, end, 0, 3 * half // 4)]),
+        (ROUTES[2], [(VALUE, end, 0, half)]),
     ]
     if kv_heads > 1:
         ways_round.append((ROUTES[3], [(VALUE, 0, 0, half)]))

time: 21.2 us -> 21.1 us (level)
  no operation moved by 1% of the time
where the time goes in v7:
time: 21.1 us; the launch traced here: 20.8 us
  Pallas kernels  20.8 us (99%)
    pallas_call x1, Pallas kernels, shards(): pl.pallas_call(kernel, out_shape=done + pending, in_specs=[pl.BlockSpec(m...  19.9 us
    pallas_call x1, Pallas kernels, shards(): pl.pallas_call(conclude, out_shape=jax.ShapeDtypeStruct((rows, q_cols), j...  0.9 us

profile of v7, /device:TPU:0, one launch (start us, length us, event | category | flops | bytes accessed | tf_op | source)
XLA Modules:
  0.0 20.8 jit_solution(17332057033923756598)
XLA Ops:
  0.0 19.9 %shard_map.46 = (bf16[256,512]{1,0:T(8,128)(2,1)S(1)}, f32[512,256]{1,0:T(8,128)S(1)}, f32[512,256]{1,0:T(8,128)S(1)}, bf16[512,256]{1,0:T(8,128)(2,1)S(1)}, bf16[256,256]{1,0:T(8,128)(2,1)S(1)}) custom-call(s32[8]{0:T(128)} %refs_0_.1, bf16[256,1024]{1,0:T(8,128)(2,1)} %refs_1_.1, bf16[256,256]{1,0:T(8,128)(2,1)} %refs_2_.1, bf16[256,256]{1,0:T(8,128)(2,1)} %refs_3_.1), custom_call_target="tpu_custom_call" | custom-call | tf_op jit(solution)/shard_map/pallas_call | solution.py:486
  19.9 0.9 %shard_map.47 = bf16[256,1024]{1,0:T(8,128)(2,1)} custom-call(f32[512,256]{1,0:T(8,128)S(1)} %get-tuple-element.10.acc_ref, f32[512,256]{1,0:T(8,128)S(1)} %get-tuple-element.11.sum_ref, bf16[512,256]{1,0:T(8,128)(2,1)S(1)} %get-tuple-element.12.p_ref, bf16[256,256]{1,0:T(8,128)(2,1)S(1)} %get-tuple-element.13.mix_ref, ...), custom_call_target="tpu_custom_call" | custom-call | tf_op jit(solution)/shard_map/pallas_call | solution.py:509
